TPU v7x, 32 devices: a whole 2x2x4 slice. The times are simulated.
32 devices in a mesh: fsdp: 4 (over y, x), ep: 8 (over z, core).
Axes of the slice: x: 2, y: 2, z: 4, core: 2. Of those that a mesh axis runs over, the one named last changes fastest.
Arguments:
- hidden_in: bfloat16 [8192, 2048], P(('fsdp', 'ep')), may hold values from -6 to 6
- norm_gain: float32 [2048], replicated, may hold values from 0.25 to 1.75
- expert_ids: int32 [8192, 8], P(('fsdp', 'ep')), may hold values from 0 to 15, all different within a row; in each aligned block of 256 rows (0 to 255, 256 to 511, ...) at most 160 rows name the same one
- expert_probs: float32 [8192, 8], P(('fsdp', 'ep')), may hold values from 0.05 to 0.25
- gate_proj: bfloat16 [16, 2048, 768], P('ep', 'fsdp'), may hold values from -0.125 to 0.125
- up_proj: bfloat16 [16, 2048, 768], P('ep', 'fsdp'), may hold values from -0.125 to 0.125
- down_proj: bfloat16 [16, 768, 2048], P('ep', None, 'fsdp'), may hold values from -0.21875 to 0.21875
Outputs:
- moe_out: bfloat16 [8192, 2048], P(('fsdp', 'ep'))
Inputs may be any that keep to these rules, and one draw needn't show every extreme that they name: `expert_ids`: within the rows of one device (aligned blocks of 256 rows) each expert id is named by at most 160 rows, and in some blocks one expert by exactly 160; the 8 ids of a row are distinct.
All inputs are finite; a program needn't handle non-finite values.
Results may differ from a plain program's by a relative error of at most 0.0025.
Values may be sent and summed in bfloat16 or wider, within the bound.
A program may use at most 128 MiB of HBM per device.

v0:
```python
import jax
import jax.numpy as jnp
from jax import lax
from jax.sharding import PartitionSpec as P


def rms_norm(hidden_in, norm_gain):
    values = hidden_in.astype(jnp.float32)
    spread = jnp.mean(values * values, axis=-1, keepdims=True)
    return (values * lax.rsqrt(spread + 1e-06) * norm_gain).astype(jnp.bfloat16)


def per_device(hidden_in, norm_gain, expert_ids, expert_probs, gate_proj, up_proj, down_proj):
    local_experts = gate_proj.shape[0]
    normed = rms_norm(hidden_in, norm_gain)
    all_experts = local_experts * lax.axis_size("ep")
    hot = expert_ids[:, :, None] == jnp.arange(all_experts, dtype=jnp.int32)
    weights = jnp.sum(jnp.where(hot, expert_probs[:, :, None], 0.0), axis=1)
    tokens = lax.all_gather(normed, "ep", axis=0, tiled=True)
    routed = lax.all_to_all(
        weights.reshape(weights.shape[0], lax.axis_size("ep"), local_experts),
        "ep",
        split_axis=1,
        concat_axis=0,
        tiled=True,
    ).reshape(tokens.shape[0], local_experts)
    total = 0.0
    gate_all = lax.all_gather(gate_proj, "fsdp", axis=1, tiled=True)
    up_all = lax.all_gather(up_proj, "fsdp", axis=1, tiled=True)
    down_all = lax.all_gather(down_proj, "fsdp", axis=2, tiled=True)
    for e in range(local_experts):
        gate = jnp.dot(tokens, gate_all[e], preferred_element_type=jnp.float32)
        up = jnp.dot(tokens, up_all[e], preferred_element_type=jnp.float32)
        act = (jax.nn.silu(gate) * up).astype(jnp.bfloat16)
        out = jnp.dot(act, down_all[e], preferred_element_type=jnp.float32).astype(jnp.bfloat16)
        total = total + out.astype(jnp.float32) * routed[:, e, None]
    combined = lax.psum_scatter(total, "ep", scatter_dimension=0, tiled=True)
    return combined.astype(jnp.bfloat16)


def solution(mesh):
    return jax.shard_map(
        per_device,
        mesh=mesh,
        in_specs=(
            P(("fsdp", "ep"), None),
            P(),
            P(("fsdp", "ep"), None),
            P(("fsdp", "ep"), None),
            P("ep", "fsdp", None),
            P("ep", "fsdp", None),
            P("ep", None, "fsdp"),
        ),
        out_specs=P(("fsdp", "ep"), None),
        check_vma=False,
    )
```

profile of v0, /device:TPU:0, one launch (start us, length us, event | category | flops | bytes accessed | tf_op | source)
XLA Modules:
  0.0 533.1 jit_solution(4729882364466384271)
XLA Ops:
  6.5 0.0 copy-start
  6.5 0.0 copy-start.1
  6.5 0.0 all-gather.7.cloned.1.call-start
  6.5 0.7 all-gather.7.cloned.1.call-update
  7.3 0.0 all-gather.5.cloned.1.call-start
  7.3 1.5 fusion.5
  8.8 2.5 fusion.7
  11.3 0.0 all-gather.5.cloned.1.call-update
  11.4 0.0 all-gather.9.cloned.1.call-start
  11.4 0.7 all-gather.9.cloned.1.call-update
  12.1 0.0 all-gather.11.cloned.1.call-start
  12.1 0.5 all-gather.11.cloned.1.call-update
  12.7 0.0 reduce-scatter.2.cloned.1.call-start
  12.7 0.0 copy-done
  12.7 0.0 copy-done.1
  12.8 11.8 %all_to_all.15 = f32[256,8,2]{0,2,1:T(2,128)S(1)} all-to-all(f32[256,8,2]{0,2,1:T(2,128)S(1)} %reshape.18), channel_id=1, replica_groups=mesh['fsdp'=4,'ep'=8] {'ep'}, dimensions={1} | all-to-all | bytes 32768 | tf_op jit(solution)/shard_map/all_to_all | solution.py:20
  24.6 57.4 %all-gather.7.cloned.1.call-done = bf16[2,2048,768]{2,1,0:T(8,128)(2,1)} async-done(((bf16[2,512,768]{2,1,0:T(8,128)(2,1)}), bf16[2,2048,768]{2,1,0:T(8,128)(2,1)}) %all-gather.7.cloned.1.call-update) | async-done | bytes 6291472 | tf_op jit(solution)/shard_map/all_gather | solution.py:28
  82.0 83.7 %all-gather.5.cloned.1.call-done = bf16[2048,2048]{1,0:T(8,128)(2,1)} async-done(((bf16[256,2048]{1,0:T(8,128)(2,1)}), bf16[2048,2048]{1,0:T(8,128)(2,1)}) %all-gather.5.cloned.1.call-update) | async-done | bytes 8388624 | tf_op jit(solution)/shard_map/all_gather | solution.py:19
  165.6 0.0 copy-start.2
  165.6 0.0 copy-start.3
  165.6 11.8 %fusion.1 = f32[2048,768]{1,0:T(8,128)} fusion(bf16[2048,2048]{1,0:T(8,128)(2,1)} %all-gather.5.cloned.1.call-done, bf16[2,2048,768]{2,1,0:T(8,128)(2,1)} %all-gather.7.cloned.1.call-done), kind=kOutput, calls=%fused_computation.7 | convolution fusion | flops 6442450944 | bytes 17825792 | tf_op jit(solution)/shard_map/dot_general | solution.py:32
  177.4 0.0 copy-done.2
  177.4 0.0 copy-done.3
  177.4 8.5 %fusion.2 = f32[2048,768]{1,0:T(8,128)} fusion(bf16[2048,2048]{1,0:T(8,128)(2,1)S(1)} %copy-done.2, bf16[2,2048,768]{2,1,0:T(8,128)(2,1)S(1)} %copy-done.3), kind=kOutput, calls=%fused_computation.11 | convolution fusion | flops 6442450944 | bytes 17825792 | tf_op jit(solution)/shard_map/dot_general | solution.py:32
  185.9 50.1 %all-gather.9.cloned.1.call-done = bf16[2,2048,768]{2,1,0:T(8,128)(2,1)} async-done(((bf16[2,512,768]{2,1,0:T(8,128)(2,1)}), bf16[2,2048,768]{2,1,0:T(8,128)(2,1)}) %all-gather.9.cloned.1.call-update) | async-done | bytes 6291472 | tf_op jit(solution)/shard_map/all_gather | solution.py:29
  236.0 71.6 %all-gather.11.cloned.1.call-done = bf16[2,768,2048]{2,1,0:T(8,128)(2,1)} async-done(((bf16[2,768,512]{2,1,0:T(8,128)(2,1)}), bf16[2,768,2048]{2,1,0:T(8,128)(2,1)}) %all-gather.11.cloned.1.call-update) | async-done | bytes 6291472 | tf_op jit(solution)/shard_map/all_gather | solution.py:30
  307.6 22.1 %fusion = bf16[2048,2048]{1,0:T(8,128)(2,1)} fusion(f32[2048,768]{1,0:T(8,128)} %fusion.2, bf16[2048,2048]{1,0:T(8,128)(2,1)} %all-gather.5.cloned.1.call-done, bf16[2,768,2048]{2,1,0:T(8,128)(2,1)} %all-gather.11.cloned.1.call-done, bf16[2,2048,768]{2,1,0:T(8,128)(2,1)} %all-gather.9.cloned.1.call-done), kind=kOutput, calls=%fused_computation.3 | convolution fusion | flops 12894339072 | bytes 29360128 | tf_op jit(solution)/shard_map/dot_general | solution.py:35
  329.7 25.8 %multiply_add_fusion = f32[2048,2048]{1,0:T(8,128)} fusion(f32[2048]{0:T(1024)S(1)} %bitcast.35, f32[2048]{0:T(1024)S(1)} %bitcast.34, bf16[2048,2048]{1,0:T(8,128)(2,1)} %fusion, f32[2048,768]{1,0:T(8,128)} %fusion.1, bf16[2048,2048]{1,0:T(8,128)(2,1)} %all-gather.5.cloned.1.call-done, bf16[2,768,2048]{2,1,0:T(8,128)(2,1)} %all-gather.11.cloned.1.call-done, ...), kind=kOutput, calls=%fused_computation | convolution fusion | flops 12919504896 | bytes 46153728 | tf_op jit(solution)/shard_map/dot_general | solution.py:35
  355.5 0.0 reduce-scatter.2.cloned.1.call-update
  355.5 168.3 %reduce-scatter.2.cloned.1.call-done = f32[256,2048]{1,0:T(8,128)} async-done(((f32[2048,2048]{1,0:T(8,128)}), f32[256,2048]{1,0:T(8,128)}) %reduce-scatter.2.cloned.1.call-update) | async-done | bytes 2097168 | tf_op jit(solution)/shard_map/reduce_scatter | solution.py:37
  523.8 2.7 convert_element_type.35
  (4 shorter events, 0.1 us)
Async XLA Ops:
  6.5 6.2 %copy-start = (f32[256,8]{0,1:T(8,128)S(1)}, f32[256,8]{0,1:T(8,128)}, u32[]{:S(2)}) copy-start(f32[256,8]{0,1:T(8,128)} %param.10) | copy-start | bytes 24580
  6.5 6.2 %copy-start.1 = (s32[256,8]{0,1:T(8,128)S(1)}, s32[256,8]{0,1:T(8,128)}, u32[]{:S(2)}) copy-start(s32[256,8]{0,1:T(8,128)} %param.9) | copy-start | bytes 24580
  6.5 75.4 %all-gather.7.cloned.1.call-start = ((), (), s32[]{:S(2)}) async-start(), calls=%async_computation.3 | async-start | bytes 7864320 | tf_op jit(solution)/shard_map/all_gather | solution.py:28
  7.3 158.4 %all-gather.5.cloned.1.call-start = ((), (), s32[]{:S(2)}) async-start(), calls=%async_computation.2 | async-start | bytes 9437184 | tf_op jit(solution)/shard_map/all_gather | solution.py:19
  11.4 224.7 %all-gather.9.cloned.1.call-start = ((), (), s32[]{:S(2)}) async-start(), calls=%async_computation.4 | async-start | bytes 7864320 | tf_op jit(solution)/shard_map/all_gather | solution.py:29
  12.1 295.5 %all-gather.11.cloned.1.call-start = ((), (), s32[]{:S(2)}) async-start(), calls=%async_computation.5 | async-start | bytes 7864320 | tf_op jit(solution)/shard_map/all_gather | solution.py:30
  12.7 511.2 %reduce-scatter.2.cloned.1.call-start = ((), (), s32[]{:S(2)}) async-start(), calls=%async_computation.6 | async-start | bytes 18874368 | tf_op jit(solution)/shard_map/reduce_scatter | solution.py:37
  165.6 11.8 %copy-start.2 = (bf16[2048,2048]{1,0:T(8,128)(2,1)S(1)}, bf16[2048,2048]{1,0:T(8,128)(2,1)}, u32[]{:S(2)}) copy-start(bf16[2048,2048]{1,0:T(8,128)(2,1)} %all-gather.5.cloned.1.call-done) | copy-start | bytes 25165828
  165.6 11.8 %copy-start.3 = (bf16[2,2048,768]{2,1,0:T(8,128)(2,1)S(1)}, bf16[2,2048,768]{2,1,0:T(8,128)(2,1)}, u32[]{:S(2)}) copy-start(bf16[2,2048,768]{2,1,0:T(8,128)(2,1)} %all-gather.7.cloned.1.call-done) | copy-start | bytes 18874372
Sparse Core Ops, SparseCore 0:
  9.2 72.7 all-gather.6
  83.6 82.0 all-gather.4
  167.5 68.5 all-gather.8
  237.7 69.8 all-gather.10
  355.6 168.1 reduce-scatter.1
where the time goes:
time: 533 us
  waiting for transfers between devices  433 us (81%)
  matrix products  68.2 us (13%)
  between operations  13.2 us (2%)
  blocking collectives  11.8 us (2%)
  other arithmetic  6.76 us (1%)
    reduce_scatter x1, waiting for transfers between devices, per_device(): combined = lax.psum_scatter(total, 'ep', scatter_dimension=0, tiled=True)  168 us
    all_gather x1, waiting for transfers between devices, per_device(): tokens = lax.all_gather(normed, 'ep', axis=0, tiled=True)  83.7 us
    all_gather x1, waiting for transfers between devices, per_device(): down_all = lax.all_gather(down_proj, 'fsdp', axis=2, tiled=True)  71.6 us
    all_gather x1, waiting for transfers between devices, per_device(): gate_all = lax.all_gather(gate_proj, 'fsdp', axis=1, tiled=True)  57.4 us
    all_gather x1, waiting for transfers between devices, per_device(): up_all = lax.all_gather(up_proj, 'fsdp', axis=1, tiled=True)  50.1 us
    dot_general x2, matrix products, per_device(): jnp.dot(act, down_all[e], preferred_element_type=jnp.float32)  47.9 us
    dot_general x2, matrix products, per_device(): gate = jnp.dot(tokens, gate_all[e], preferred_element_type=jnp.float32)  20.3 us
    all_to_all x1, blocking collectives, per_device(): lax.all_to_all(weights.reshape(weights.shape[0], lax.axis_size('ep'), loc...  11.8 us
  transfers between devices with their start and end apart: 5, of which 5 were waited for; matrix products, arithmetic and copies ran while one was open for 5% of the time, Pallas kernels for 0%

commit v1 on v0

--- a/solution.py
+++ b/solution.py
@@ -25,7 +25,12 @@
         tiled=True,
     ).reshape(tokens.shape[0], local_experts)
     total = 0.0
-    gate_all = lax.all_gather(gate_proj, "fsdp", axis=1, tiled=True)
+    ring = [gate_proj]
+    for hop in range(3):
+        ring.append(lax.ppermute(ring[-1], "fsdp", [(dev, (dev + 1) % 4) for dev in range(4)]))
+    gate_all = jnp.roll(
+        jnp.concatenate(ring[::-1], axis=1), (lax.axis_index("fsdp") + 1) * ring[0].shape[1], axis=1
+    )
     up_all = lax.all_gather(up_proj, "fsdp", axis=1, tiled=True)
     down_all = lax.all_gather(down_proj, "fsdp", axis=2, tiled=True)
     for e in range(local_experts):

time: 533 us -> 478 us (0.90)
  waiting for transfers between devices: 433 us -> 363 us
  local copies, waits for them, and re-layouts: 0.04 us -> 16.5 us
  blocking collectives: 11.8 us -> 0 us
  starting transfers between devices: 0.16 us -> 8.71 us
    ppermute x0 -> x3, waiting for transfers between devices: none -> 113 us  [per_device(): lax.ppermute(ring[-1], 'fsdp', [(dev, (dev + 1) % 4) for dev in range(4)])]
    all_gather x1, waiting for transfers between devices: 83.7 us -> 0.01 us  [per_device(): tokens = lax.all_gather(normed, 'ep', axis=0, tiled=True)]
    all_gather x1 -> x0, waiting for transfers between devices: 57.4 us -> none  [per_device(): gate_all = lax.all_gather(gate_proj, 'fsdp', axis=1, tiled=True)]
    all_gather x1, waiting for transfers between devices: 50.1 us -> 2.54 us  [per_device(): up_all = lax.all_gather(up_proj, 'fsdp', axis=1, tiled=True)]
    unnamed x8 -> x15, local copies, waits for them, and re-layouts: 0.01 us -> 14.6 us
    all_to_all x1 -> x0, blocking collectives: 11.8 us -> none  [per_device(): lax.all_to_all(weights.reshape(weights.shape[0], lax.axis_size('ep'), loc...]
    all_to_all x0 -> x1, waiting for transfers between devices: none -> 5.59 us  [per_device(): lax.all_to_all(weights.reshape(weights.shape[0], lax.axis_size('ep'), loc...]
  transfers between devices with their start and end apart: 5 -> 8, of which waited for: 5 -> 7; matrix products, arithmetic and copies ran while one was open for 5% -> 8% of each run, Pallas kernels for 0% -> 0%
where the time goes in v1:
time: 478 us
  waiting for transfers between devices  363 us (76%)
  matrix products  70 us (15%)
  local copies, waits for them, and re-layouts  16.5 us (3%)
  between operations  13.2 us (3%)
  starting transfers between devices  8.71 us (2%)
  other arithmetic  6.88 us (1%)
    reduce_scatter x1, waiting for transfers between devices, per_device(): combined = lax.psum_scatter(total, 'ep', scatter_dimension=0, tiled=True)  168 us
    ppermute x3, waiting for transfers between devices, per_device(): lax.ppermute(ring[-1], 'fsdp', [(dev, (dev + 1) % 4) for dev in range(4)])  113 us
    all_gather x1, waiting for transfers between devices, per_device(): down_all = lax.all_gather(down_proj, 'fsdp', axis=2, tiled=True)  71.8 us
    dot_general x2, matrix products, per_device(): jnp.dot(act, down_all[e], preferred_element_type=jnp.float32)  47.9 us
    dot_general x2, matrix products, per_device(): gate = jnp.dot(tokens, gate_all[e], preferred_element_type=jnp.float32)  22.1 us
    unnamed x15, local copies, waits for them, and re-layouts  14.6 us
  transfers between devices with their start and end apart: 8, of which 7 were waited for; matrix products, arithmetic and copies ran while one was open for 8% of the time, Pallas kernels for 0%

profile of v1, /device:TPU:0, one launch (start us, length us, event | category | flops | bytes accessed | tf_op | source)
XLA Modules:
  0.0 477.9 jit_solution(8513453567276228162)
XLA Ops:
  6.5 0.0 copy-start
  6.5 0.0 copy-start.1
  6.5 0.0 copy-start.2
  6.5 0.0 all-gather.4.cloned.1.call-start
  6.5 1.6 fusion.9
  8.2 2.5 fusion.11
  10.7 0.0 all-gather.4.cloned.1.call-update
  10.7 0.0 all-gather.6.cloned.1.call-start
  10.8 0.7 all-gather.6.cloned.1.call-update
  11.5 0.0 all-gather.8.cloned.1.call-start
  11.5 0.7 all-gather.8.cloned.1.call-update
  12.2 0.0 copy-done
  12.2 3.0 collective-permute-start
  15.2 35.3 %collective-permute-done = bf16[2,512,768]{2,1,0:T(8,128)(2,1)S(1)} collective-permute-done((bf16[2,512,768]{2,1,0:T(8,128)(2,1)S(1)}, bf16[2,512,768]{2,1,0:T(8,128)(2,1)S(1)}, u32[]{:S(2)}, u32[]{:S(2)}) %collective-permute-start) | collective-permute-done | bytes 1572896 | tf_op jit(solution)/shard_map/ppermute | solution.py:30
  50.6 0.8 collective-permute-start.1
  51.4 35.9 %collective-permute-done.1 = bf16[2,512,768]{2,1,0:T(8,128)(2,1)} collective-permute-done((bf16[2,512,768]{2,1,0:T(8,128)(2,1)S(1)}, bf16[2,512,768]{2,1,0:T(8,128)(2,1)}, u32[]{:S(2)}, u32[]{:S(2)}) %collective-permute-start.1) | collective-permute-done | bytes 1572896 | tf_op jit(solution)/shard_map/ppermute | solution.py:30
  87.2 0.0 collective-permute-start.2
  87.3 0.0 copy-done.1
  87.3 0.0 copy-done.2
  87.3 0.6 reshape.18
  87.9 4.8 %all-to-all-start = ((f32[256,8,2]{0,2,1:T(2,128)}), f32[256,8,2]{0,2,1:T(2,128)S(1)}, u32[]{:S(2)}, u32[]{:S(2)}) async-start(f32[256,8,2]{0,2,1:T(2,128)} %reshape.18), calls=%async_computation | async-start | bytes 32768 | tf_op jit(solution)/shard_map/all_to_all | solution.py:20
  92.7 0.0 reduce-scatter.2.cloned.1.call-start
  92.8 5.6 %all-to-all-done = f32[256,8,2]{0,2,1:T(2,128)S(1)} async-done(((f32[256,8,2]{0,2,1:T(2,128)}), f32[256,8,2]{0,2,1:T(2,128)S(1)}, u32[]{:S(2)}, u32[]{:S(2)}) %all-to-all-start) | async-done | bytes 16416 | tf_op jit(solution)/shard_map/all_to_all | solution.py:20
  98.4 41.8 %collective-permute-done.2 = bf16[2,512,768]{2,1,0:T(8,128)(2,1)} collective-permute-done((bf16[2,512,768]{2,1,0:T(8,128)(2,1)}, bf16[2,512,768]{2,1,0:T(8,128)(2,1)}, u32[]{:S(2)}, u32[]{:S(2)}) %collective-permute-start.2) | collective-permute-done | bytes 1572896 | tf_op jit(solution)/shard_map/ppermute | solution.py:30
  140.1 2.7 constant_dynamic-update-slice_fusion.7
  142.8 2.7 constant_dynamic-update-slice_fusion.6
  145.5 1.3 constant_dynamic-update-slice_fusion.5
  146.8 1.3 constant_dynamic-update-slice_fusion.4
  148.1 2.7 constant_dynamic-update-slice_fusion.3
  150.7 2.7 constant_dynamic-update-slice_fusion.2
  153.4 1.3 constant_dynamic-update-slice_fusion.1
  154.7 1.2 constant_dynamic-update-slice_fusion
  156.0 0.0 all-gather.4.cloned.1.call-done
  156.0 0.0 copy-start.3
  156.0 11.8 %fusion.5 = f32[2048,768]{1,0:T(8,128)} fusion(bf16[2048,2048]{1,0:T(8,128)(2,1)} %all-gather.4.cloned.1.call-done, bf16[2,4096,768]{2,1,0:T(8,128)(2,1)} %constant_dynamic-update-slice_fusion, s32[]{:T(128)S(6)} %add.44, s32[]{:T(128)S(6)} %select_n.18), kind=kOutput, calls=%fused_computation.9 | convolution fusion | flops 6442450944 | bytes 17825800 | tf_op jit(solution)/shard_map/dot_general | solution.py:37
  167.7 0.0 copy-done.3
  167.7 10.3 %fusion.6 = f32[2048,768]{1,0:T(8,128)} fusion(bf16[2048,2048]{1,0:T(8,128)(2,1)S(1)} %copy-done.3, bf16[2,4096,768]{2,1,0:T(8,128)(2,1)} %constant_dynamic-update-slice_fusion, s32[]{:T(128)S(6)} %select_n.18), kind=kOutput, calls=%fused_computation.13 | convolution fusion | flops 6442450944 | bytes 17825796 | tf_op jit(solution)/shard_map/dot_general | solution.py:37
  178.1 2.5 all-gather.6.cloned.1.call-done
  180.6 71.8 %all-gather.8.cloned.1.call-done = bf16[2,768,2048]{2,1,0:T(8,128)(2,1)} async-done(((bf16[2,768,512]{2,1,0:T(8,128)(2,1)}), bf16[2,768,2048]{2,1,0:T(8,128)(2,1)}) %all-gather.8.cloned.1.call-update) | async-done | bytes 6291472 | tf_op jit(solution)/shard_map/all_gather | solution.py:35
  252.4 22.2 %fusion = bf16[2048,2048]{1,0:T(8,128)(2,1)} fusion(f32[2048,768]{1,0:T(8,128)} %fusion.6, bf16[2048,2048]{1,0:T(8,128)(2,1)} %all-gather.4.cloned.1.call-done, bf16[2,768,2048]{2,1,0:T(8,128)(2,1)} %all-gather.8.cloned.1.call-done, bf16[2,2048,768]{2,1,0:T(8,128)(2,1)} %all-gather.6.cloned.1.call-done), kind=kOutput, calls=%fused_computation.3 | convolution fusion | flops 12894339072 | bytes 29360128 | tf_op jit(solution)/shard_map/dot_general | solution.py:40
  274.5 25.8 %multiply_add_fusion = f32[2048,2048]{1,0:T(8,128)} fusion(f32[2048]{0:T(1024)S(1)} %bitcast.35, f32[2048]{0:T(1024)S(1)} %bitcast.34, bf16[2048,2048]{1,0:T(8,128)(2,1)} %fusion, f32[2048,768]{1,0:T(8,128)} %fusion.5, bf16[2048,2048]{1,0:T(8,128)(2,1)} %all-gather.4.cloned.1.call-done, bf16[2,768,2048]{2,1,0:T(8,128)(2,1)} %all-gather.8.cloned.1.call-done, ...), kind=kOutput, calls=%fused_computation | convolution fusion | flops 12919504896 | bytes 46153728 | tf_op jit(solution)/shard_map/dot_general | solution.py:40
  300.3 0.0 reduce-scatter.2.cloned.1.call-update
  300.3 168.3 %reduce-scatter.2.cloned.1.call-done = f32[256,2048]{1,0:T(8,128)} async-done(((f32[2048,2048]{1,0:T(8,128)}), f32[256,2048]{1,0:T(8,128)}) %reduce-scatter.2.cloned.1.call-update) | async-done | bytes 2097168 | tf_op jit(solution)/shard_map/reduce_scatter | solution.py:42
  468.6 2.7 convert_element_type.35
  (3 shorter events, 0.0 us)
Async XLA Ops:
  6.5 5.7 %copy-start = (bf16[2,512,768]{2,1,0:T(8,128)(2,1)S(1)}, bf16[2,512,768]{2,1,0:T(8,128)(2,1)}, u32[]{:S(2)}) copy-start(bf16[2,512,768]{2,1,0:T(8,128)(2,1)} %param.11) | copy-start | bytes 4718596
  6.5 80.7 %copy-start.1 = (f32[256,8]{0,1:T(8,128)S(1)}, f32[256,8]{0,1:T(8,128)}, u32[]{:S(2)}) copy-start(f32[256,8]{0,1:T(8,128)} %param.10) | copy-start | bytes 24580
  6.5 80.7 %copy-start.2 = (s32[256,8]{0,1:T(8,128)S(1)}, s32[256,8]{0,1:T(8,128)}, u32[]{:S(2)}) copy-start(s32[256,8]{0,1:T(8,128)} %param.9) | copy-start | bytes 24580
  6.5 149.4 %all-gather.4.cloned.1.call-start = ((), (), s32[]{:S(2)}) async-start(), calls=%async_computation.2 | async-start | bytes 9437184 | tf_op jit(solution)/shard_map/all_gather | solution.py:19
  10.7 169.9 %all-gather.6.cloned.1.call-start = ((), (), s32[]{:S(2)}) async-start(), calls=%async_computation.3 | async-start | bytes 7864320 | tf_op jit(solution)/shard_map/all_gather | solution.py:34
  11.5 240.9 %all-gather.8.cloned.1.call-start = ((), (), s32[]{:S(2)}) async-start(), calls=%async_computation.4 | async-start | bytes 7864320 | tf_op jit(solution)/shard_map/all_gather | solution.py:35
  12.2 38.4 %collective-permute-start = (bf16[2,512,768]{2,1,0:T(8,128)(2,1)S(1)}, bf16[2,512,768]{2,1,0:T(8,128)(2,1)S(1)}, u32[]{:S(2)}, u32[]{:S(2)}) collective-permute-start(bf16[2,512,768]{2,1,0:T(8,128)(2,1)S(1)} %copy-done), channel_id=1, source_target_pairs={{0,8},{8,16},{16,24},{24,0},{1,9},{9,17},{17,25},{25,1},{2,10},{10... | collective-permute-start | bytes 4718600 | tf_op jit(solution)/shard_map/ppermute | solution.py:30
  50.6 36.7 %collective-permute-start.1 = (bf16[2,512,768]{2,1,0:T(8,128)(2,1)S(1)}, bf16[2,512,768]{2,1,0:T(8,128)(2,1)}, u32[]{:S(2)}, u32[]{:S(2)}) collective-permute-start(bf16[2,512,768]{2,1,0:T(8,128)(2,1)S(1)} %collective-permute-done), channel_id=1, source_target_pairs={{0,8},{8,16},{16,24},{24,0},{1,9},{9,17},{17,25},{25,1},{2,10},{10... | collective-permute-start | bytes 4718600 | tf_op jit(solution)/shard_map/ppermute | solution.py:30
  87.2 52.9 %collective-permute-start.2 = (bf16[2,512,768]{2,1,0:T(8,128)(2,1)}, bf16[2,512,768]{2,1,0:T(8,128)(2,1)}, u32[]{:S(2)}, u32[]{:S(2)}) collective-permute-start(bf16[2,512,768]{2,1,0:T(8,128)(2,1)} %collective-permute-done.1), channel_id=1, source_target_pairs={{0,8},{8,16},{16,24},{24,0},{1,9},{9,17},{17,25},{25,1},{2,10},{10... | collective-permute-start | bytes 4718600 | tf_op jit(solution)/shard_map/ppermute | solution.py:30
  87.9 10.4 %all-to-all-start = ((f32[256,8,2]{0,2,1:T(2,128)}), f32[256,8,2]{0,2,1:T(2,128)S(1)}, u32[]{:S(2)}, u32[]{:S(2)}) async-start(f32[256,8,2]{0,2,1:T(2,128)} %reshape.18), calls=%async_computation | async-start | bytes 32768 | tf_op jit(solution)/shard_map/all_to_all | solution.py:20
  92.7 375.9 %reduce-scatter.2.cloned.1.call-start = ((), (), s32[]{:S(2)}) async-start(), calls=%async_computation.5 | async-start | bytes 18874368 | tf_op jit(solution)/shard_map/reduce_scatter | solution.py:42
  156.0 11.8 %copy-start.3 = (bf16[2048,2048]{1,0:T(8,128)(2,1)S(1)}, bf16[2048,2048]{1,0:T(8,128)(2,1)}, u32[]{:S(2)}) copy-start(bf16[2048,2048]{1,0:T(8,128)(2,1)} %all-gather.4.cloned.1.call-done) | copy-start | bytes 25165828
Sparse Core Ops, SparseCore 0:
  10.8 84.7 all-gather.3
  97.5 83.1 all-gather.5
  182.5 69.8 all-gather.7
  300.4 168.1 reduce-scatter.1
